TPU v7x, 32 devices: a whole 2x2x4 slice. The times are simulated.
32 devices in a mesh: rep: 2 (over y), span: 2 (over core), seq: 4 (over z), tp: 2 (over x).
Axes of the slice: x: 2, y: 2, z: 4, core: 2. Of those that a mesh axis runs over, the one named last changes fastest.
Arguments:
- queries: bfloat16 [8, 512, 24, 128], P(('rep', 'span'), 'seq', 'tp'), parts along dimension 0, may hold values from -110 to 110
- key_states: bfloat16 [8, 512, 4, 128], P(('rep', 'span'), 'seq', 'tp'), parts along dimension 0, may hold values from -11 to 11
- value_states: bfloat16 [8, 512, 4, 128], P(('rep', 'span'), 'seq', 'tp'), parts along dimension 0, may hold values from -6 to 6
- out_weight: bfloat16 [3072, 6144], P('tp', 'seq'), may hold values from -0.109375 to 0.109375
- noise_table: float32 [64, 6144], P(None, 'tp'), may hold values from 0.5 to 2
- plan: int32 [8], P('rep'), parts along dimension 0, may hold values from 0 to 63
Outputs:
- branch_out: bfloat16 [8, 512, 6144], P(('rep', 'span'), 'seq', 'tp'), parts along dimension 0
There are 2 independent parts, one for each index of `rep`. A program takes and returns all parts, laid end to end along the dimension named above; an argument that names none is the same for every part. Nothing has to cross between parts.
All inputs are finite; a program needn't handle non-finite values.
Results may differ from a plain program's by a relative error of at most 0.014.
Values may be sent and summed in bfloat16 or wider, within the bound.
A program may use at most 128 MiB of HBM per device.

v0:
```python
import jax
import jax.numpy as jnp
from jax import lax
from jax.sharding import PartitionSpec as P


def fold_block(carried, query_rows, key_rows, value_rows, factor):
    maxima, totals, weighted = carried
    scores = (
        jnp.einsum("tkgd,skd->tkgs", query_rows, key_rows, preferred_element_type=jnp.float32)
        * factor
    )
    highest = jnp.maximum(maxima, jnp.max(scores, axis=-1))
    shrink = jnp.exp(maxima - highest)
    weights = jnp.exp(scores - highest[..., None])
    totals = totals * shrink + jnp.sum(weights, axis=-1)
    weighted = weighted * shrink[..., None] + jnp.einsum(
        "tkgs,skd->tkgd",
        weights.astype(jnp.bfloat16),
        value_rows,
        preferred_element_type=jnp.float32,
    )
    return (maxima * 0.0 + highest, totals, weighted)


def per_device(queries, key_states, value_states, out_weight, noise_table, plan):
    ch_dev, tok_dev, heads_local, head_size = queries.shape
    kv_local = key_states.shape[2]
    per_kv = heads_local // kv_local
    span_count = ch_dev * lax.axis_size("span")
    first_span = lax.axis_index("span") * ch_dev
    factor = head_size ** (-0.5)
    grouped = queries.reshape(ch_dev, tok_dev, kv_local, per_kv, head_size)
    start_max = jnp.full((ch_dev, tok_dev, kv_local, per_kv), -1e30, jnp.float32)
    start_tot = jnp.zeros((ch_dev, tok_dev, kv_local, per_kv), jnp.float32)
    start_acc = jnp.zeros((ch_dev, tok_dev, kv_local, per_kv, head_size), jnp.float32)
    span_rows = (
        lax.all_gather(key_states, "seq", axis=1, tiled=True),
        lax.all_gather(value_states, "seq", axis=1, tiled=True),
    )
    key_piece = lax.all_gather(span_rows[0], "span", axis=0, tiled=True)
    value_piece = lax.all_gather(span_rows[1], "span", axis=0, tiled=True)
    new_max = []
    new_tot = []
    new_acc = []
    for q_span in range(ch_dev):
        inner_state = (start_max[q_span], start_tot[q_span], start_acc[q_span])
        for k_span in range(span_count):

            def update(inner, q_span=q_span, k_span=k_span):
                return fold_block(
                    inner, grouped[q_span], key_piece[k_span], value_piece[k_span], factor
                )

            inner_state = lax.cond(
                k_span <= first_span + q_span, update, lambda inner: inner, inner_state
            )
        new_max.append(inner_state[0])
        new_tot.append(inner_state[1])
        new_acc.append(inner_state[2])
    attn = (
        (jnp.stack(new_acc) / jnp.stack(new_tot)[..., None])
        .reshape(ch_dev, tok_dev, heads_local * head_size)
        .astype(jnp.bfloat16)
    )
    columns = jnp.einsum(
        "ctf,fo->cto",
        lax.all_gather(attn, "seq", axis=1, tiled=True),
        out_weight,
        preferred_element_type=jnp.float32,
    )
    partial_out = lax.all_to_all(
        columns.astype(jnp.bfloat16), "seq", split_axis=1, concat_axis=2, tiled=True
    ).astype(columns.dtype)
    summed = lax.psum_scatter(
        partial_out.astype(jnp.bfloat16), "tp", scatter_dimension=2, tiled=True
    ).astype(jnp.float32)
    levels = lax.dynamic_slice_in_dim(plan, first_span, ch_dev)
    picks = (levels[:, None] == jnp.arange(noise_table.shape[0], dtype=jnp.int32)[None, :]).astype(
        jnp.float32
    )
    gates = jnp.dot(picks, noise_table, precision=lax.Precision.HIGHEST)
    return (summed * gates[:, None, :]).astype(jnp.bfloat16)


def solution(mesh):
    placed = (
        P(("rep", "span"), "seq", "tp", None),
        P(("rep", "span"), "seq", "tp", None),
        P(("rep", "span"), "seq", "tp", None),
        P("tp", "seq"),
        P(None, "tp"),
        P("rep"),
    )
    return jax.shard_map(
        per_device,
        mesh=mesh,
        in_specs=placed,
        out_specs=P(("rep", "span"), "seq", "tp"),
        check_vma=False,
    )
```

profile of v0, /device:TPU:0, one launch (start us, length us, event | category | flops | bytes accessed | tf_op | source)
XLA Modules:
  0.0 320.5 jit_solution(18199733619609409647)
XLA Ops:
  6.5 1.0 copy.63
  7.5 18.0 %all_gather.15 = bf16[2,512,2,128]{3,1,2,0:T(8,128)(2,1)} all-gather(bf16[2,128,2,128]{3,1,2,0:T(8,128)(2,1)S(1)} %copy.63), channel_id=1, replica_groups=mesh['rep'=2,'span'=2,'seq'=4,'tp'=2] {'seq'}, dimensions={1}, use_global_device_ids=true | all-gather | bytes 655360 | tf_op jit(solution)/shard_map/all_gather | solution.py:38
  25.6 0.9 copy.64
  26.5 17.0 %all_gather.17 = bf16[2,512,2,128]{3,1,2,0:T(8,128)(2,1)} all-gather(bf16[2,128,2,128]{3,1,2,0:T(8,128)(2,1)S(1)} %copy.64), channel_id=1, replica_groups=mesh['rep'=2,'span'=2,'seq'=4,'tp'=2] {'seq'}, dimensions={1}, use_global_device_ids=true | all-gather | bytes 655360 | tf_op jit(solution)/shard_map/all_gather | solution.py:39
  43.7 9.6 %all-gather.6.cloned.1.call-done = bf16[4,512,2,128]{3,1,2,0:T(8,128)(2,1)} async-done(((bf16[2,512,2,128]{3,1,2,0:T(8,128)(2,1)}), bf16[4,512,2,128]{3,1,2,0:T(8,128)(2,1)}) %all-gather.6.cloned.1.call-update) | async-done | bytes 1048592 | tf_op jit(solution)/shard_map/all_gather | solution.py:42
  53.3 6.1 %conditional.12 = (f32[128,2,6]{0,2,1:T(8,128)}, f32[128,2,6]{0,2,1:T(8,128)S(1)}, f32[128,2,6,128]{3,0,2,1:T(8,128)S(1)}) conditional(s32[]{:T(128)} %convert_element_type.70, () %tuple.93, (bf16[4,512,2,128]{3,1,2,0:T(8,128)(2,1)}, bf16[2,128,2,6,128]{4,1,3,2,0:T(8,128)(2,1)}, bf16[4,512,2,128]{3,1,2,0:T(8,128)(2,1)}) %tuple.190), branch_computations={%region_16.0_spmd, %region_17.0_spmd} | conditional | flops 409147392 | bytes 11210776 | solution.py:55
  53.3 1.7 bitcast_reduce_fusion.4
  55.6 1.2 fusion.85
  56.8 0.7 fusion.104
  57.5 1.9 fusion.93
  59.4 6.2 %conditional.13 = ((f32[128,2,6]{0,2,1:T(8,128)}, f32[128,2,6]{0,2,1:T(8,128)S(1)}, f32[128,2,6,128]{3,0,2,1:T(8,128)S(1)})) conditional(s32[]{:T(128)} %convert_element_type.69, (f32[128,2,6]{0,2,1:T(8,128)}, f32[128,2,6]{0,2,1:T(8,128)S(1)}, f32[128,2,6,128]{3,0,2,1:T(8,128)S(1)}) %conditional.12, (f32[128,2,6]{0,2,1:T(8,128)}, ...), branch_computations={%region_20.0_spmd, %region_21.0_spmd} | conditional | flops 409344000 | bytes 12032032 | solution.py:55
  59.4 1.7 bitcast_reduce_fusion.5
  62.3 0.7 multiply_add_fusion.4
  63.6 2.0 fusion.115
  65.6 6.1 %conditional.8 = (f32[128,2,6]{0,2,1:T(8,128)}, f32[128,2,6]{0,2,1:T(8,128)S(1)}, f32[128,2,6,128]{3,0,2,1:T(8,128)S(1)}) conditional(s32[]{:T(128)} %convert_element_type.66, () %tuple.87, (bf16[4,512,2,128]{3,1,2,0:T(8,128)(2,1)}, bf16[2,128,2,6,128]{4,1,3,2,0:T(8,128)(2,1)}, bf16[4,512,2,128]{3,1,2,0:T(8,128)(2,1)}) %tuple.193), branch_computations={%region_0.0_spmd, %region_1.0_spmd} | conditional | flops 409147392 | bytes 11210776 | solution.py:55
  65.6 1.7 bitcast_reduce_fusion
  67.9 1.2 fusion.2
  69.8 1.9 fusion.10
  72.0 1.5 conditional.15
  72.2 1.2 copy.102
  73.4 1.4 conditional.11
  73.7 1.2 copy.100
  75.0 1.6 copy.73
  76.6 2.9 fusion.171
  79.6 93.0 %all-gather.8.cloned.1.call-done = bf16[2,512,1536]{2,1,0:T(8,128)(2,1)} async-done(((bf16[2,128,1536]{2,1,0:T(8,128)(2,1)}), bf16[2,512,1536]{2,1,0:T(8,128)(2,1)}) %all-gather.8.cloned.1.call-update) | async-done | bytes 3145744 | tf_op jit(solution)/shard_map/all_gather | solution.py:68
  172.6 8.1 %fusion.168 = bf16[2,512,1536]{2,1,0:T(8,128)(2,1)S(1)} fusion(bf16[2,512,1536]{2,1,0:T(8,128)(2,1)} %all-gather.8.cloned.1.call-done, bf16[1536,1536]{1,0:T(8,128)(2,1)} %param.25), kind=kOutput, calls=%fused_computation.166 | convolution fusion | flops 4833411072 | bytes 11010048 | tf_op jit(solution)/shard_map/ctf,fo->cto/dot_general | solution.py:66
  180.7 3.2 %copy.74 = bf16[2,512,1536]{2,0,1:T(2,128)(2,1)S(1)} copy(bf16[2,512,1536]{2,1,0:T(8,128)(2,1)S(1)} %fusion.168) | data formatting | bytes 6291456 | tf_op jit(solution)/shard_map/convert_element_type | solution.py:73
  183.9 73.3 %all_to_all.18 = bf16[2,512,1536]{2,0,1:T(2,128)(2,1)S(1)} all-to-all(bf16[2,512,1536]{2,0,1:T(2,128)(2,1)S(1)} %copy.74), channel_id=1, replica_groups=mesh['rep'=2,'span'=2,'seq'=4,'tp'=2] {'seq'}, dimensions={1} | all-to-all | bytes 6291456 | tf_op jit(solution)/shard_map/all_to_all | solution.py:72
  257.2 4.1 %copy.75 = bf16[2,128,4,1536]{3,2,1,0:T(4,128)(2,1)} copy(bf16[2,128,4,1536]{3,0,1,2:T(2,128)(2,1)S(1)} %bitcast.326) | data formatting | bytes 6291456 | tf_op jit(solution)/shard_map/all_to_all | solution.py:72
  261.3 6.9 %all_to_all.16 = bf16[2,128,6144]{2,1,0:T(8,128)(2,1)} reshape(bf16[2,128,4,1536]{3,2,1,0:T(4,128)(2,1)} %copy.75) | data formatting | bytes 6291456 | tf_op jit(solution)/shard_map/all_to_all | solution.py:72
  269.4 41.7 %reduce-scatter.2.cloned.1.call-done = bf16[2,128,3072]{2,1,0:T(8,128)(2,1)} async-done(((bf16[2,128,6144]{2,1,0:T(8,128)(2,1)}), bf16[2,128,3072]{2,1,0:T(8,128)(2,1)}) %reduce-scatter.2.cloned.1.call-update) | async-done | bytes 1572880 | tf_op jit(solution)/shard_map/reduce_scatter | solution.py:75
  311.1 2.9 multiply_convert_fusion
  (28 shorter events, 5.9 us)
Async XLA Ops:
  6.5 262.4 %copy-start = (f32[64,3072]{1,0:T(8,128)S(1)}, f32[64,3072]{1,0:T(8,128)}, u32[]{:S(2)}) copy-start(f32[64,3072]{1,0:T(8,128)} %param.26) | copy-start | bytes 2359300
  6.5 37.2 %all-gather.4.cloned.1.call-start = ((), (), s32[]{:S(2)}) async-start(), calls=%async_computation.2 | async-start | bytes 1572864 | tf_op jit(solution)/shard_map/all_gather | solution.py:41
  25.6 27.7 %all-gather.6.cloned.1.call-start = ((), (), s32[]{:S(2)}) async-start(), calls=%async_computation.3 | async-start | bytes 1572864 | tf_op jit(solution)/shard_map/all_gather | solution.py:42
  43.6 129.0 %all-gather.8.cloned.1.call-start = ((), (), s32[]{:S(2)}) async-start(), calls=%async_computation.4 | async-start | bytes 3932160 | tf_op jit(solution)/shard_map/all_gather | solution.py:68
  79.6 231.5 %reduce-scatter.2.cloned.1.call-start = ((), (), s32[]{:S(2)}) async-start(), calls=%async_computation.5 | async-start | bytes 4718592 | tf_op jit(solution)/shard_map/reduce_scatter | solution.py:75
  268.3 0.7 copy-start.5
Sparse Core Ops, SparseCore 0:
  25.7 10.8 all-gather.3
  43.7 9.5 all-gather.5
  79.7 92.8 all-gather.7
  268.4 42.6 reduce-scatter.1
where the time goes:
time: 322 us; the launch traced here: 321 us
  waiting for transfers between devices  144 us (45%)
  blocking collectives  108 us (34%)
  local copies, waits for them, and re-layouts  22.1 us (7%)
  matrix products  19.2 us (6%)
  between operations  13.2 us (4%)
  other arithmetic  12.9 us (4%)
    all_gather x1, waiting for transfers between devices, per_device(): lax.all_gather(attn, 'seq', axis=1, tiled=True)  93 us
    all_to_all x1, blocking collectives, per_device(): lax.all_to_all(columns.astype(jnp.bfloat16), 'seq', split_axis=1, concat_...  73.3 us
    reduce_scatter x1, waiting for transfers between devices, per_device(): lax.psum_scatter(partial_out.astype(jnp.bfloat16), 'tp', scatter_dimensio...  41.7 us
    all_gather x1, blocking collectives, per_device(): lax.all_gather(key_states, 'seq', axis=1, tiled=True)  18 us
    all_gather x1, blocking collectives, per_device(): lax.all_gather(value_states, 'seq', axis=1, tiled=True)  17 us
    all_to_all x2, local copies, waits for them, and re-layouts, per_device(): lax.all_to_all(columns.astype(jnp.bfloat16), 'seq', split_axis=1, concat_...  11 us
    all_gather x1, waiting for transfers between devices, per_device(): value_piece = lax.all_gather(span_rows[1], 'span', axis=0, tiled=True)  9.6 us
    dot_general x1, matrix products, per_device(): jnp.einsum('ctf,fo->cto', lax.all_gather(attn, 'seq', axis=1, tiled=True)...  8.06 us
  transfers between devices with their start and end apart: 4, of which 3 were waited for; matrix products, arithmetic and copies ran while one was open for 0% of the time, Pallas kernels for 0%

commit v1 on v0

--- a/solution.py
+++ b/solution.py
@@ -2,6 +2,37 @@
 import jax.numpy as jnp
 from jax import lax
 from jax.sharding import PartitionSpec as P
+
+
+def resolve_ratios(local_x, row_axis, u_in):
+    reply = lax.axis_size(row_axis)
+    raw_out = lax.axis_index(row_axis)
+    right_arr, response, clean = (reply, raw_out, local_x.shape[1])
+    series = [(m, (m + 1) % right_arr) for m in range(right_arr)]
+    made = [(ii, dev_j) for dev_j, ii in series]
+    y2 = lax.ppermute(local_x, row_axis, series)
+    row_out = lax.ppermute(local_x, row_axis, made)
+    outcome_arr, r2 = (y2, row_out)
+    p_next = u_in(local_x, response * clean)
+    local_next = p_next.shape[1]
+    o_now = jnp.zeros((*p_next.shape[:1], right_arr * local_next, *p_next.shape[2:]), p_next.dtype)
+
+    def create_ratios_on(o_now, p_next, f_next):
+        return lax.dynamic_update_slice_in_dim(o_now, p_next, f_next * local_next, axis=1)
+
+    o_now = create_ratios_on(o_now, p_next, response)
+    for b in range(1, right_arr // 2 + 1):
+        q_next, block_last = ((response - b) % right_arr, (response + b) % right_arr)
+        fresh = (outcome_arr, r2)
+        if b < right_arr // 2:
+            carry = lax.ppermute(outcome_arr, row_axis, series)
+            long_array = lax.ppermute(r2, row_axis, made)
+            outcome_arr, r2 = (carry, long_array)
+        later = u_in(fresh[0], q_next * clean)
+        o_now = create_ratios_on(o_now, later, q_next)
+        if 2 * b < right_arr:
+            o_now = create_ratios_on(o_now, u_in(fresh[1], block_last * clean), block_last)
+    return o_now
 
 
 def fold_block(carried, query_rows, key_rows, value_rows, factor):
@@ -63,11 +94,12 @@
         .reshape(ch_dev, tok_dev, heads_local * head_size)
         .astype(jnp.bfloat16)
     )
-    columns = jnp.einsum(
-        "ctf,fo->cto",
-        lax.all_gather(attn, "seq", axis=1, tiled=True),
-        out_weight,
-        preferred_element_type=jnp.float32,
+    columns = resolve_ratios(
+        attn,
+        "seq",
+        u_in=lambda own_block, start: jnp.einsum(
+            "ctf,fo->cto", own_block, out_weight, preferred_element_type=jnp.float32
+        ),
     )
     partial_out = lax.all_to_all(
         columns.astype(jnp.bfloat16), "seq", split_axis=1, concat_axis=2, tiled=True

time: 322 us -> 264 us (0.82)
  waiting for transfers between devices: 144 us -> 101 us
  blocking collectives: 108 us -> 93.1 us
  starting transfers between devices: 0.13 us -> 3.96 us
    all_gather x1 -> x0, waiting for transfers between devices: 93 us -> none  [per_device(): lax.all_gather(attn, 'seq', axis=1, tiled=True)]
    reduce_scatter x1, waiting for transfers between devices: 41.7 us -> 75.5 us  [per_device(): lax.psum_scatter(partial_out.astype(jnp.bfloat16), 'tp', scatter_dimensio...]
    ppermute x0 -> x3, waiting for transfers between devices: none -> 16 us  [the longest x1 6.23 us: resolve_ratios(): carry = lax.ppermute(outcome_arr, row_axis, series)]
    all_to_all x1, blocking collectives: 73.3 us -> 58.1 us  [per_device(): lax.all_to_all(columns.astype(jnp.bfloat16), 'seq', split_axis=1, concat_...]
    all_to_all x2, local copies, waits for them, and re-layouts: 11 us -> 6.8 us  [per_device(): lax.all_to_all(columns.astype(jnp.bfloat16), 'seq', split_axis=1, concat_...]
    ppermute x0 -> x3, starting transfers between devices: none -> 3.88 us  [the longest x1 2.07 us: resolve_ratios(): row_out = lax.ppermute(local_x, row_axis, made)]
    dynamic_update_slice x0 -> x4, local copies, waits for them, and re-layouts: none -> 3.55 us  [create_ratios_on(): lax.dynamic_update_slice_in_dim(o_now, p_next, f_next * local_next, axis=1)]
    dot_general x1 -> x4, matrix products: 8.06 us -> 7.84 us  [per_device(): jnp.einsum('ctf,fo->cto', own_block, out_weight, preferred_element_type=j...]
  transfers between devices with their start and end apart: 4 -> 6, of which waited for: 3 -> 5; matrix products, arithmetic and copies ran while one was open for 0% -> 5% of each run, Pallas kernels for 0% -> 0%
where the time goes in v1:
time: 264 us; the launch traced here: 263 us
  waiting for transfers between devices  101 us (38%)
  blocking collectives  93.1 us (35%)
  local copies, waits for them, and re-layouts  21.4 us (8%)
  matrix products  19 us (7%)
  between operations  13.3 us (5%)
  other arithmetic  11.1 us (4%)
  starting transfers between devices  3.96 us (2%)
    reduce_scatter x1, waiting for transfers between devices, per_device(): lax.psum_scatter(partial_out.astype(jnp.bfloat16), 'tp', scatter_dimensio...  75.5 us
    all_to_all x1, blocking collectives, per_device(): lax.all_to_all(columns.astype(jnp.bfloat16), 'seq', split_axis=1, concat_...  58.1 us
    all_gather x1, blocking collectives, per_device(): lax.all_gather(key_states, 'seq', axis=1, tiled=True)  18 us
    all_gather x1, blocking collectives, per_device(): lax.all_gather(value_states, 'seq', axis=1, tiled=True)  17 us
    all_gather x1, waiting for transfers between devices, per_device(): value_piece = lax.all_gather(span_rows[1], 'span', axis=0, tiled=True)  9.54 us
    dot_general x4, matrix products, per_device(): jnp.einsum('ctf,fo->cto', own_block, out_weight, preferred_element_type=j...  7.84 us
    all_to_all x2, local copies, waits for them, and re-layouts, per_device(): lax.all_to_all(columns.astype(jnp.bfloat16), 'seq', split_axis=1, concat_...  6.8 us
    ppermute x1, waiting for transfers between devices, resolve_ratios(): carry = lax.ppermute(outcome_arr, row_axis, series)  6.23 us
  transfers between devices with their start and end apart: 6, of which 5 were waited for; matrix products, arithmetic and copies ran while one was open for 5% of the time, Pallas kernels for 0%

profile of v1, /device:TPU:0, one launch (start us, length us, event | category | flops | bytes accessed | tf_op | source)
XLA Modules:
  0.0 263.1 jit_solution(16729916723101127039)
XLA Ops:
  7.5 18.0 %all_gather.12 = bf16[2,512,2,128]{3,1,2,0:T(8,128)(2,1)} all-gather(bf16[2,128,2,128]{3,1,2,0:T(8,128)(2,1)S(1)} %copy.86), channel_id=1, replica_groups=mesh['rep'=2,'span'=2,'seq'=4,'tp'=2] {'seq'}, dimensions={1}, use_global_device_ids=true | all-gather | bytes 655360 | tf_op jit(solution)/shard_map/all_gather | solution.py:69
  26.5 17.0 %all_gather.14 = bf16[2,512,2,128]{3,1,2,0:T(8,128)(2,1)} all-gather(bf16[2,128,2,128]{3,1,2,0:T(8,128)(2,1)S(1)} %copy.87), channel_id=1, replica_groups=mesh['rep'=2,'span'=2,'seq'=4,'tp'=2] {'seq'}, dimensions={1}, use_global_device_ids=true | all-gather | bytes 655360 | tf_op jit(solution)/shard_map/all_gather | solution.py:70
  43.8 9.5 %all-gather.5.cloned.1.call-done = bf16[4,512,2,128]{3,1,2,0:T(8,128)(2,1)} async-done(((bf16[2,512,2,128]{3,1,2,0:T(8,128)(2,1)}), bf16[4,512,2,128]{3,1,2,0:T(8,128)(2,1)}) %all-gather.5.cloned.1.call-update) | async-done | bytes 1048592 | tf_op jit(solution)/shard_map/all_gather | solution.py:73
  53.3 6.1 %conditional.8 = (f32[128,2,6]{0,2,1:T(8,128)}, f32[128,2,6]{0,2,1:T(8,128)S(1)}, f32[128,2,6,128]{3,0,2,1:T(8,128)S(1)}) conditional(s32[]{:T(128)} %convert_element_type.66, () %tuple.87, (bf16[4,512,2,128]{3,1,2,0:T(8,128)(2,1)}, bf16[2,128,2,6,128]{4,1,3,2,0:T(8,128)(2,1)}, bf16[4,512,2,128]{3,1,2,0:T(8,128)(2,1)}) %tuple.198), branch_computations={%region_0.0_spmd, %region_1.0_spmd} | conditional | flops 409147392 | bytes 11210776 | solution.py:86
  53.3 1.7 bitcast_reduce_fusion
  55.6 1.2 fusion.2
  57.5 1.9 fusion.10
  59.4 6.1 %conditional.12 = (f32[128,2,6]{0,2,1:T(8,128)}, f32[128,2,6]{0,2,1:T(8,128)S(1)}, f32[128,2,6,128]{3,0,2,1:T(8,128)S(1)}) conditional(s32[]{:T(128)} %convert_element_type.70, () %tuple.93, (bf16[4,512,2,128]{3,1,2,0:T(8,128)(2,1)}, bf16[2,128,2,6,128]{4,1,3,2,0:T(8,128)(2,1)}, bf16[4,512,2,128]{3,1,2,0:T(8,128)(2,1)}) %tuple.201), branch_computations={%region_16.0_spmd, %region_17.0_spmd} | conditional | flops 409147392 | bytes 11210776 | solution.py:86
  59.4 1.7 bitcast_reduce_fusion.4
  63.6 1.9 fusion.93
  65.5 6.2 %conditional.13 = ((f32[128,2,6]{0,2,1:T(8,128)}, f32[128,2,6]{0,2,1:T(8,128)S(1)}, f32[128,2,6,128]{3,0,2,1:T(8,128)S(1)})) conditional(s32[]{:T(128)} %convert_element_type.69, (f32[128,2,6]{0,2,1:T(8,128)}, f32[128,2,6]{0,2,1:T(8,128)S(1)}, f32[128,2,6,128]{3,0,2,1:T(8,128)S(1)}) %conditional.12, (f32[128,2,6]{0,2,1:T(8,128)}, ...), branch_computations={%region_20.0_spmd, %region_21.0_spmd} | conditional | flops 409344000 | bytes 12032032 | solution.py:86
  65.5 1.7 bitcast_reduce_fusion.5
  69.1 2.0 fusion.115
  71.8 1.5 conditional.11
  74.8 1.6 copy.96
  76.4 2.0 fusion.174
  78.4 1.8 collective-permute-start
  80.2 2.1 collective-permute-start.1
  82.3 3.7 %fusion.172 = bf16[2,128,1536]{2,1,0:T(8,128)(2,1)S(1)} fusion(bf16[2,128,1536]{2,1,0:T(8,128)(2,1)S(1)} %fusion.174, bf16[1536,1536]{1,0:T(8,128)(2,1)} %param.25), kind=kOutput, calls=%fused_computation.170 | convolution fusion | flops 1207959552 | bytes 6291456 | tf_op jit(solution)/shard_map/ctf,fo->cto/dot_general | solution.py:100
  86.0 1.6 broadcast_in_dim.2
  88.5 3.8 %collective-permute-done = bf16[2,128,1536]{2,1,0:T(8,128)(2,1)S(1)} collective-permute-done((bf16[2,128,1536]{2,1,0:T(8,128)(2,1)S(1)}, bf16[2,128,1536]{2,1,0:T(8,128)(2,1)S(1)}, u32[]{:S(2)}, u32[]{:S(2)}) %collective-permute-start) | collective-permute-done | bytes 786464 | tf_op jit(solution)/shard_map/ppermute | solution.py:13
  92.4 1.4 fusion.170
  94.6 6.0 %collective-permute-done.1 = bf16[2,128,1536]{2,1,0:T(8,128)(2,1)S(1)} collective-permute-done((bf16[2,128,1536]{2,1,0:T(8,128)(2,1)S(1)}, bf16[2,128,1536]{2,1,0:T(8,128)(2,1)S(1)}, u32[]{:S(2)}, u32[]{:S(2)}) %collective-permute-start.1) | collective-permute-done | bytes 786464 | tf_op jit(solution)/shard_map/ppermute | solution.py:14
  100.6 1.4 fusion.168
  102.9 6.2 %collective-permute-done.2 = bf16[2,128,1536]{2,1,0:T(8,128)(2,1)S(1)} collective-permute-done((bf16[2,128,1536]{2,1,0:T(8,128)(2,1)S(1)}, bf16[2,128,1536]{2,1,0:T(8,128)(2,1)S(1)}, u32[]{:S(2)}, u32[]{:S(2)}) %collective-permute-start.2) | collective-permute-done | bytes 786464 | tf_op jit(solution)/shard_map/ppermute | solution.py:28
  109.1 1.4 fusion.166
  111.4 58.1 %all_to_all.18 = bf16[2,512,1536]{2,0,1:T(2,128)(2,1)S(1)} all-to-all(bf16[2,512,1536]{2,0,1:T(2,128)(2,1)S(1)} %copy_dynamic-update-slice_fusion), channel_id=1, replica_groups=mesh['rep'=2,'span'=2,'seq'=4,'tp'=2] {'seq'}, dimensions={1} | all-to-all | bytes 6291456 | tf_op jit(solution)/shard_map/all_to_all | solution.py:104
  169.5 2.2 copy.101
  171.7 4.6 %copy.102 = bf16[2,128,4,1536]{1,3,2,0:T(8,128)(2,1)} copy(bf16[2,128,4,1536]{3,1,2,0:T(8,128)(2,1)} %bitcast.335) | data formatting | bytes 6291456 | tf_op jit(solution)/shard_map/all_to_all | solution.py:104
  177.4 75.5 %reduce-scatter.2.cloned.1.call-done = bf16[2,128,3072]{1,2,0:T(8,128)(2,1)} async-done(((bf16[2,128,6144]{1,2,0:T(8,128)(2,1)}), bf16[2,128,3072]{1,2,0:T(8,128)(2,1)}) %reduce-scatter.2.cloned.1.call-update) | async-done | bytes 1572880 | tf_op jit(solution)/shard_map/reduce_scatter | solution.py:107
  252.9 2.1 multiply_convert_fusion
  255.0 1.6 copy.103
  (48 shorter events, 16.6 us)
Async XLA Ops:
  6.5 170.5 %copy-start = (f32[64,3072]{1,0:T(8,128)S(1)}, f32[64,3072]{1,0:T(8,128)}, u32[]{:S(2)}) copy-start(f32[64,3072]{1,0:T(8,128)} %param.26) | copy-start | bytes 2359300
  6.5 37.2 %all-gather.3.cloned.1.call-start = ((), (), s32[]{:S(2)}) async-start(), calls=%async_computation.2 | async-start | bytes 1572864 | tf_op jit(solution)/shard_map/all_gather | solution.py:72
  25.6 27.7 %all-gather.5.cloned.1.call-start = ((), (), s32[]{:S(2)}) async-start(), calls=%async_computation.3 | async-start | bytes 1572864 | tf_op jit(solution)/shard_map/all_gather | solution.py:73
  43.6 209.3 %reduce-scatter.2.cloned.1.call-start = ((), (), s32[]{:S(2)}) async-start(), calls=%async_computation.4 | async-start | bytes 4718592 | tf_op jit(solution)/shard_map/reduce_scatter | solution.py:107
  73.8 0.9 copy-start.5
  74.7 1.7 copy-start.6
  76.4 16.0 %slice-start = ((s8[4718592]{0:T(1024)(128)(4,1)}), s8[4194304]{0:T(1024)(128)(4,1)S(1)}, s32[]{:S(2)}) async-start(s8[4718592]{0:T(1024)(128)(4,1)} %bitcast.343), calls=%async_computation.5 | async-start | bytes 8388608
  78.4 14.0 %slice-start.1 = ((s8[4718592]{0:T(1024)(128)(4,1)}), s8[524288]{0:T(1024)(128)(4,1)S(1)}, s32[]{:S(2)}) async-start(s8[4718592]{0:T(1024)(128)(4,1)} %bitcast.343), calls=%async_computation.6 | async-start | bytes 1048576
  78.4 13.9 %collective-permute-start = (bf16[2,128,1536]{2,1,0:T(8,128)(2,1)S(1)}, bf16[2,128,1536]{2,1,0:T(8,128)(2,1)S(1)}, u32[]{:S(2)}, u32[]{:S(2)}) collective-permute-start(bf16[2,128,1536]{2,1,0:T(8,128)(2,1)S(1)} %fusion.174), channel_id=1, source_target_pairs={{0,2},{2,4},{4,6},{6,0},{1,3},{3,5},{5,7},{7,1},{8,10},{10,12},{12... | collective-permute-start | bytes 2359304 | tf_op jit(solution)/shard_map/ppermute | solution.py:13
  80.2 20.4 %collective-permute-start.1 = (bf16[2,128,1536]{2,1,0:T(8,128)(2,1)S(1)}, bf16[2,128,1536]{2,1,0:T(8,128)(2,1)S(1)}, u32[]{:S(2)}, u32[]{:S(2)}) collective-permute-start(bf16[2,128,1536]{2,1,0:T(8,128)(2,1)S(1)} %fusion.174), channel_id=1, source_target_pairs={{2,0},{4,2},{6,4},{0,6},{3,1},{5,3},{7,5},{1,7},{10,8},{12,10},{14... | collective-permute-start | bytes 2359304 | tf_op jit(solution)/shard_map/ppermute | solution.py:14
  92.3 16.8 %collective-permute-start.2 = (bf16[2,128,1536]{2,1,0:T(8,128)(2,1)S(1)}, bf16[2,128,1536]{2,1,0:T(8,128)(2,1)S(1)}, u32[]{:S(2)}, u32[]{:S(2)}) collective-permute-start(bf16[2,128,1536]{2,1,0:T(8,128)(2,1)S(1)} %collective-permute-done), channel_id=1, source_target_pairs={{0,2},{2,4},{4,6},{6,0},{1,3},{3,5},{5,7},{7,1},{8,10},{10,12},{12... | collective-permute-start | bytes 2359304 | tf_op jit(solution)/shard_map/ppermute | solution.py:28
  176.3 0.7 copy-start.7
Sparse Core Ops, SparseCore 0:
  25.7 10.8 all-gather.2
  43.7 9.5 all-gather.4
  176.5 76.3 reduce-scatter.1
